TPU v7x, 32 devices: a 4x4x1 block of a 4x4x8 slice. The times are simulated.
32 devices in a mesh: member: 1 (over z), ty: 4 (over y), tx: 4 (over x), panel: 2 (over core).
Axes of the slice: x: 4, y: 4, z: 1, core: 2. Of those that a mesh axis runs over, the one named last changes fastest.
The devices are a block of a 4x4x8 slice.
Arguments:
- height: float32 [6, 768, 768], P(('member', 'panel'), 'tx', 'ty')
- wind_u: float32 [6, 768, 768], P(('member', 'panel'), 'tx', 'ty')
- wind_v: float32 [6, 768, 768], P(('member', 'panel'), 'tx', 'ty')
- sqrt_g: float32 [6, 768, 768], P('panel', 'tx', 'ty')
- metric_aa: float32 [6, 768, 768], P('panel', 'tx', 'ty')
- metric_ab: float32 [6, 768, 768], P('panel', 'tx', 'ty')
- metric_bb: float32 [6, 768, 768], P('panel', 'tx', 'ty')
- coriolis: float32 [6, 768, 768], P('panel', 'tx', 'ty')
- topography: float32 [6, 768, 768], P('panel', 'tx', 'ty')
- rotation: float32 [6, 4, 768, 2, 2], P('panel')
- tracers: float32 [8, 6, 768, 768], P(None, ('member', 'panel'), 'tx', 'ty')
Outputs:
- output 1: float32 [6, 768, 768], P(('member', 'panel'), 'tx', 'ty')
- output 2: float32 [6, 768, 768], P(('member', 'panel'), 'tx', 'ty')
- output 3: float32 [6, 768, 768], P(('member', 'panel'), 'tx', 'ty')
- output 4: float32 [8, 6, 768, 768], P(None, ('member', 'panel'), 'tx', 'ty')
All inputs are finite; a program needn't handle non-finite values.
Results may differ from a plain program's by a relative error of at most 0.001.
Values sent between devices are 32-bit elements.
A program may use at most 768 MiB of HBM per device.

v0:
```python
import functools

import jax
import jax.numpy as jnp
from jax import lax
from jax.experimental import pallas as pl
from jax.experimental.pallas import tpu as pltpu
from jax.sharding import PartitionSpec as P

STEPS = 8
TIME_STEP = 0.1
GRAVITY = 1.0
WAVE_SPEED = 1.0
LINKS = (
    '310 100 530 420',
    '010 200 511 410',
    '110 300 521 431',
    '210 000 500 401',
    '331 130 030 231',
    '320 121 221 020',
)
NEIGHBOURS = tuple(tuple(tuple(map(int, link)) for link in row.split()) for row in LINKS)
LANES = 128
HALF = 96
TOP = 8
EDGES = 4
BASE = 3
DEPTH = 2
ROWS1 = 16
ROWS2 = 16
ROWSB = 32
ROWSP = 32
F32 = jnp.float32


def pick(index, values):
    if all(value is values[0] for value in values):
        return values[0]
    total = 0
    for place, value in enumerate(values):
        total = total + same(index, place) * value
    return total


def same(x, y):
    return 1 - lax.min((x - y) * (x - y), 1)


def mix(cond, yes, no):
    return cond * yes + (1 - cond) * no


def on_edge(edge, along, count):
    if edge == 0:
        return 0, along
    if edge == 1:
        return count - 1, along
    if edge == 2:
        return along, 0
    return along, count - 1


class Plan:
    def __init__(self, core, pos_a, pos_b, cores, count):
        self.core, self.pos_a, self.pos_b = core, pos_a, pos_b
        self.cores, self.count = cores, count
        self.slots = 6 // cores
        first = lambda x: 1 - lax.div(x + count - 1, count)
        last = lambda x: lax.div(x + 1, count)
        self.at_edge = (first(pos_a), last(pos_a), first(pos_b), last(pos_b))

    def across(self, slot, edge, along, side=None):
        found = []
        for core in range(self.cores):
            other, other_edge, flipped = NEIGHBOURS[core * self.slots + slot][edge]
            place = self.count - 1 - along if flipped else along
            tile_a, tile_b = on_edge(other_edge, place, self.count)
            if side is None:
                index = (other % self.slots) * EDGES + other_edge
            else:
                end = 1 - side if flipped else side
                if other_edge < 2:
                    index = (other % self.slots) * EDGES + 2 * other_edge + end
                else:
                    index = (other % self.slots) * EDGES + 2 * end + other_edge - 2
            found.append((other // self.slots, tile_a, tile_b, index))
        return tuple(pick(self.core, [entry[k] for entry in found]) for k in range(EDGES))

    def edge(self, slot, edge):
        along = self.pos_b if edge < 2 else self.pos_a
        out = self.across(slot, edge, along)
        step = 1 if edge % 2 else -1
        inside = (
            self.core,
            self.pos_a + (step if edge < 2 else 0),
            self.pos_b + (0 if edge < 2 else step),
            slot * EDGES + (edge ^ 1),
        )
        return tuple(mix(self.at_edge[edge], o, i) for o, i in zip(out, inside))

    def corner(self, slot, end_a, end_b):
        step_a, step_b = 2 * end_a - 1, 2 * end_b - 1
        out_a, out_b = self.at_edge[end_a], self.at_edge[2 + end_b]
        by_a = self.across(slot, end_a, self.pos_b + step_b, 1 - end_b)
        by_b = self.across(slot, 2 + end_b, self.pos_a + step_a, 1 - end_a)
        inside = (self.core, self.pos_a + step_a, self.pos_b + step_b, slot * EDGES + 2 * (1 - end_a) + 1 - end_b)
        return tuple(mix(out_a, x, mix(out_b, y, z)) for x, y, z in zip(by_a, by_b, inside))

    def lone(self, end_a, end_b):
        return self.at_edge[end_a] * self.at_edge[2 + end_b]

    def here(self, found):
        return same(found[0], self.core) * same(found[1], self.pos_a) * same(found[2], self.pos_b)

    def can_stay(self, slot, edge):
        for core in range(self.cores):
            other, other_edge, flipped = NEIGHBOURS[core * self.slots + slot][edge]
            if other // self.slots == core:
                for along in range(self.count):
                    place = self.count - 1 - along if flipped else along
                    if on_edge(edge, along, self.count) == on_edge(other_edge, place, self.count):
                        return True
        return False

    def flip(self, slot, edge):
        values = [NEIGHBOURS[core * self.slots + slot][edge][2] for core in range(self.cores)]
        if not any(values):
            return None
        return self.at_edge[edge] * pick(self.core, values)


def roll(x, shift, axis):
    shift = shift % x.shape[axis]
    return x if shift == 0 else pltpu.roll(x, shift, axis)


def kernel(cores, count, tile, height, wind_u, wind_v, sqrt_g, metric_aa, metric_ab, metric_bb, coriolis,
           topography, coef_e, coef_c, tracers, out_h, out_u, out_v, out_q,
           dyn_a, dyn_b, tra_a, tra_b, stat, area, aux, coef, pack, ghost_t, ghost_d, ghost_q,
           *traffic):
    slots = 6 // cores
    fields = tracers.shape[0]
    plan = Plan(lax.axis_index('panel'), lax.axis_index('tx'), lax.axis_index('ty'), cores, count)
    edges = [[plan.edge(s, e) for e in range(EDGES)] for s in range(slots)]
    corners = [[plan.corner(s, k // 2, k % 2) for k in range(EDGES)] for s in range(slots)]
    lone = [plan.lone(k // 2, k % 2) for k in range(EDGES)]
    stays = [[plan.here(edges[s][e]) if plan.can_stay(s, e) else None for e in range(EDGES)] for s in range(slots)]
    lanes = lambda rows: lax.broadcasted_iota(jnp.int32, (rows, LANES), 1)
    lane = lanes(1)
    lane8 = lax.broadcasted_iota(jnp.int32, (8, LANES), 1)
    even8 = lax.broadcasted_iota(jnp.int32, (8, LANES), 0) % 2 == 0
    last_lane = tile - LANES - 1
    inner = pl.ds(TOP, tile)
    one = lambda k: pl.ds(k, 1)

    def where_to(found):
        return {'panel': found[0], 'tx': found[1], 'ty': found[2]}

    of_dyn, of_tra, of_end = (traffic[k::BASE] for k in range(BASE))

    def start(kind, par, index, found, stay=None):
        send, recv, spare, sent, landed = kind

        def away():
            pltpu.make_async_remote_copy(
                src_ref=send.at[par, index], dst_ref=recv.at[par, found[-1]], send_sem=sent.at[par],
                recv_sem=landed.at[par], device_id=where_to(found), device_id_type=pl.DeviceIdType.MESH).start()

        def inside():
            pltpu.make_async_copy(send.at[par, index], recv.at[par, found[-1]], landed.at[par]).start()
            pltpu.make_async_copy(send.at[par, index], spare.at[par, index], sent.at[par]).start()
        if stay is None:
            away()
        else:
            pl.when(stay == 0)(away)
            pl.when(stay == 1)(inside)

    def wait_for(kind, par):
        send, recv, _, sent, landed = kind
        pltpu.make_async_copy(recv.at[par], recv.at[par], landed.at[par]).wait()
        pltpu.make_async_copy(send.at[par], send.at[par], sent.at[par]).wait()

    of_end[1][...] = jnp.zeros_like(of_end[1])
    barrier = pltpu.get_barrier_semaphore()
    expected = 0
    for s in range(slots):
        for e in range(EDGES):
            stay = 0 if stays[s][e] is None else stays[s][e]

            def tell(s=s, e=e):
                pl.semaphore_signal(barrier, inc=1, device_id=where_to(edges[s][e]), device_id_type=pl.DeviceIdType.MESH)
            if stays[s][e] is None:
                tell()
            else:
                pl.when(stay == 0)(tell)
            expected = expected + 1 - stay
        for k in range(EDGES):
            @pl.when(lone[k] == 0)
            def _(s=s, k=k):
                pl.semaphore_signal(barrier, inc=1, device_id=where_to(corners[s][k]), device_id_type=pl.DeviceIdType.MESH)
            expected = expected + 1 - lone[k]

    def swap_pairs(x):
        return jnp.where(even8, roll(x, -1, 0), roll(x, 1, 0))

    def send_all(kind, par):
        for s in range(slots):
            for e in range(EDGES):
                start(kind, par, EDGES * s + e, edges[s][e], stays[s][e])

    def pack_columns(src, count_f, depth, send, par):
        def step(i, carry):
            r0 = pl.multiple_of(ROWSP * i, ROWSP)
            rows = pl.ds(r0 + TOP, ROWSP)
            lane = lanes(ROWSP)
            packed = jnp.zeros((ROWSP, LANES), F32)
            for s in range(slots):
                for f in range(count_f):
                    low = DEPTH * TOP * s + depth * f
                    high = low + TOP
                    x = roll(src(s)[f, 0, rows, :], low, 1)
                    packed = jnp.where((lane >= low) & (lane < low + depth), x, packed)
                    x = roll(src(s)[f, 1, rows, :], high - last_lane + depth - 1, 1)
                    packed = jnp.where((lane >= high) & (lane < high + depth), x, packed)
            pack[pl.ds(r0, ROWSP), :] = packed
            return carry
        lax.fori_loop(0, tile // ROWSP, step, 0)
        turned0 = jnp.transpose(pack[:LANES])
        turned1 = jnp.transpose(pack[LANES:])
        for s in range(slots):
            for side in range(DEPTH):
                g = TOP * (DEPTH * s + side)
                left = turned0[g:g + TOP]
                right = jnp.where(lane8 < tile - LANES, turned1[g:g + TOP], left)
                if side and depth == DEPTH:
                    left, right = swap_pairs(left), swap_pairs(right)
                index = EDGES * s + DEPTH + side
                send[par, index, 0] = left
                send[par, index, 1] = right

    def pack_rows(src, count_f, depth, send, par):
        for s in range(slots):
            for f in range(count_f):
                for d in range(depth):
                    k = one(depth * f + d)
                    send[par, EDGES * s, :, k, :] = src(s)[f, :, one(TOP + d), :]
                    send[par, EDGES * s + 1, :, k, :] = src(s)[f, :, one(tile + TOP - 1 - d), :]

    def send_corners(src, par):
        send = of_end[0]
        for s in range(slots):
            for k in range(EDGES):
                end_a, end_b = divmod(k, DEPTH)
                row = tile + TOP - 1 if end_a else TOP
                at = last_lane if end_b else 0
                for f in range(1, BASE):
                    cell = src(s)[f, end_b, one(row), one(at)]
                    send[par, EDGES * s + k, one(f - 1), :] = jnp.broadcast_to(cell, (1, LANES))
        for s in range(slots):
            for k in range(EDGES):
                found = corners[s][k]
                mine = EDGES * s + k
                start(of_end, par, mine, found[:-1] + (mix(lone[k], mine, found[-1]),), lone[k])

    def unpack(dst, count_f, depth, kind, par, ghosts, turn):
        recv = kind[1]
        wait_for(kind, par)
        ends = {}
        for s in range(slots):
            for e in range(EDGES):
                index = EDGES * s + e
                left, right = recv[par, index, 0], recv[par, index, 1]
                flip = plan.flip(s, e)
                if flip is not None:
                    flipped = (jnp.zeros_like(lane8) + flip) == 1
                    mirror = lane8 ^ last_lane
                    back = jnp.take_along_axis(right, mirror, axis=1)
                    forth = jnp.take_along_axis(left, mirror, axis=1)
                    left, right = jnp.where(flipped, back, left), jnp.where(flipped, forth, right)
                if turn:
                    both = []
                    for lr, x in enumerate((left, right)):
                        stay, down, up = (coef_e[index, lr, k] for k in range(BASE))
                        both.append(stay * x + down * roll(x, DEPTH, 0) + up * roll(x, -DEPTH, 0))
                    left, right = both
                if e < DEPTH:
                    for f in range(count_f):
                        for d in range(depth):
                            k = depth * f + d
                            row = one(tile + TOP + d if e else TOP - 1 - d)
                            dst(s)[f, 0, row, :] = left[k:k + 1]
                            dst(s)[f, 1, row, :] = right[k:k + 1]
                    ends[s, e] = (left, right)
                else:
                    if e == DEPTH and depth == DEPTH:
                        left, right = swap_pairs(left), swap_pairs(right)
                    g = pl.ds(TOP * (DEPTH * s + e - DEPTH), TOP)
                    ghost_t[0, g, :] = jnp.where(lane8 < HALF, left, right)
                    ghost_t[1, g, :] = right
        low = jnp.transpose(ghost_t[0])
        high = jnp.transpose(ghost_t[1])[:tile - LANES]
        for s in range(slots):
            shift = -DEPTH * TOP * s
            ghosts[s, pl.ds(TOP, LANES), :] = roll(low, shift, 1)
            ghosts[s, pl.ds(TOP + LANES, tile - LANES), :] = roll(high, shift, 1)
        return ends

    def unpack_corners(par, ends):
        wait_for(of_end, par)
        for s in range(slots):
            rows = [jnp.zeros((1, LANES), F32)] * DEPTH
            for k in range(EDGES):
                end_a, end_b = divmod(k, DEPTH)
                x = of_end[1][par, EDGES * s + k]
                stay, down, up = (coef_c[EDGES * s + k, j] for j in range(BASE))
                x = stay * x + down * roll(x, 1, 0) + up * roll(x, -1, 0)
                alone = (jnp.zeros_like(lane) + lone[k]) == 1
                edge_row = ends[s, end_a][end_b]
                at = last_lane if end_b else 0
                for f in range(1, BASE):
                    mirrored = jnp.broadcast_to(edge_row[DEPTH * f:DEPTH * f + 1, at:at + 1], (1, LANES))
                    value = jnp.where(alone, mirrored, x[f - 1:f])
                    place = DEPTH * f + (TOP if end_b else 1)
                    rows[end_a] = jnp.where(lane == place, value, rows[end_a])
            ghost_d[s, one(TOP - 1), :] = rows[0]
            ghost_d[s, one(tile + TOP), :] = rows[1]

    def exchanged(left, right):
        lane = lanes(left.shape[0])
        return (jnp.where((lane == HALF) | (lane == HALF + 1), right, left),
                jnp.where((lane == HALF - 1) | (lane == HALF - 2), left, right))

    def with_columns(x, ghosts, low):
        left, right = exchanged(x[0], x[1])
        lane = lanes(left.shape[0])
        left = jnp.where(lane >= LANES - 2, roll(ghosts, LANES - 2 - low, 1), left)
        ghosts = roll(ghosts, tile - LANES - low - 8, 1)
        right = jnp.where((lane == tile - LANES) | (lane == tile - LANES + 1), ghosts, right)
        return jnp.stack([left, right])

    def take(src, dst):
        dst[0, inner, :] = src[:, :LANES]
        dst[1, inner, :] = roll(src[:, tile - LANES:], tile - LANES, 1)

    zero_rows = jnp.zeros((2 * LANES - tile, LANES), F32)
    pack[tile:2 * LANES, :] = zero_rows
    ghost_t[...] = jnp.zeros_like(ghost_t)
    ghost_d[...] = jnp.zeros_like(ghost_d)
    ghost_q[...] = jnp.zeros_like(ghost_q)
    for kind in (of_dyn, of_end):
        kind[0][...] = jnp.zeros_like(kind[0])
    group0 = lambda s: stat.at[s, 0]
    group1 = lambda s: stat.at[s, 1]
    def take_state(s, carry):
        for k, ref in enumerate((sqrt_g, metric_aa, metric_ab)):
            take(ref.at[s], stat.at[s, 0, k])
        for k, ref in enumerate((metric_bb, topography, coriolis)):
            take(ref.at[s], stat.at[s, 1, k])
        for k, ref in enumerate((height, wind_u, wind_v)):
            take(ref.at[s], dyn_a.at[s, k])
        return carry
    lax.fori_loop(0, slots, take_state, 0)
    dyn_of = {0: lambda s: dyn_a.at[s], 1: lambda s: dyn_b.at[s]}
    tra_of = {0: lambda s: tra_a.at[s], 1: lambda s: tra_b.at[s]}
    groups = (DEPTH, group0), (BASE, group1)
    for par, group in groups:
        pack_columns(group, BASE, DEPTH, of_dyn[0], par)
        pack_rows(group, BASE, DEPTH, of_dyn[0], par)
        if par == DEPTH:
            pl.semaphore_wait(barrier, expected)
        send_all(of_dyn, par)

    def pack_dyn(par):
        pack_columns(dyn_of[par], BASE, DEPTH, of_dyn[0], par)
        pack_rows(dyn_of[par], BASE, DEPTH, of_dyn[0], par)
        send_all(of_dyn, par)
        send_corners(dyn_of[par], par)

    def pack_tra(par):
        pack_columns(tra_of[par], fields, 1, of_tra[0], par)
        pack_rows(tra_of[par], fields, 1, of_tra[0], par)
        send_all(of_tra, par)

    pack_dyn(0)
    def take_tracer(t, carry):
        for s in range(slots):
            take(tracers.at[t, s], tra_a.at[s, t])
        return carry
    lax.fori_loop(0, fields, take_tracer, 0)
    pack_tra(0)

    for par, group in groups:
        unpack(group, BASE, DEPTH, of_dyn, par, ghost_d, False)
        def fill_slot(s, carry):
            def fill(i, carry):
                rows = pl.ds(pl.multiple_of(ROWSP * i, ROWSP) + 8, ROWSP)
                g = ghost_d[s, rows, :]
                for f in range(3):
                    group(s)[f, :, rows, :] = with_columns(group(s)[f, :, rows, :], g, 2 * f)
                if par == DEPTH:
                    inverse = 1.0 / group(s)[0, :, rows, :]
                    area[s, 0, :, rows, :] = inverse
                    area[s, 1, :, rows, :] = (-0.5 * TIME_STEP) * inverse
                return carry
            return lax.fori_loop(0, tile // ROWSP, fill, carry)
        lax.fori_loop(0, slots, fill_slot, 0)

    def first_pass(s, now):
        state = dyn_of[now](s)

        def step(i, carry):
            rows = pl.ds(pl.multiple_of(ROWS1 * i, ROWS1), ROWS1)
            g = ghost_d[s, rows, :]
            h, u, v = (with_columns(state[f, :, rows, :], g, 2 * f) for f in range(3))
            state[0, :, rows, :] = h
            state[1, :, rows, :] = u
            state[2, :, rows, :] = v
            jac, gaa, gab = (stat[s, 0, k, :, rows, :] for k in range(3))
            gbb, top = (stat[s, 1, k, :, rows, :] for k in range(2))
            contra_a = gaa * u + gab * v
            contra_b = gab * u + gbb * v
            jh = jac * h
            aux[0, :, rows, :] = GRAVITY * (h + top) + 0.5 * (u * contra_a + v * contra_b)
            aux[1, :, rows, :] = jh * contra_a
            aux[2, :, rows, :] = jh * contra_b
            aux[3, :, rows, :] = contra_a
            aux[4, :, rows, :] = contra_b
            return carry
        lax.fori_loop(0, (tile + 16) // ROWS1, step, 0)

    def second_pass(s, now):
        state, fresh = dyn_of[now](s), dyn_of[1 - now](s)

        def step(i, carry):
            r0 = pl.multiple_of(ROWS2 * i, 8) + 8

            def at(ref, f, shift=0):
                return ref[f, :, pl.ds(r0 + shift, ROWS2), :]
            rows = pl.ds(r0, ROWS2)
            h, u, v = (at(state, f) for f in range(3))
            area_here = area.at[s]
            inv_jac = at(area_here, 0)
            jac = at(stat.at[s, 0], 0)
            mass_a = at(aux, 1)
            plus, minus = mass_a + h, mass_a - h
            flux_e = plus + (at(aux, 1, 1) - at(state, 0, 1))
            flux_w = (at(aux, 1, -1) + at(state, 0, -1)) + minus
            mass_b = at(aux, 2)
            flux_n = (mass_b + h) + roll(mass_b - h, -1, 2)
            flux_s = roll(flux_n, 1, 2)
            total = (flux_e - flux_w) + (flux_n - flux_s)
            h_t = (-0.5) * total * inv_jac
            coef[s, 0, :, rows, :] = 0.5 * total + 4.0
            coef[s, 1, :, rows, :] = 0.5 * flux_e - 1.0
            coef[s, 2, :, rows, :] = -0.5 * flux_w - 1.0
            coef[s, 3, :, rows, :] = 0.5 * flux_n - 1.0
            coef[s, 4, :, rows, :] = -0.5 * flux_s - 1.0
            twelfth = 1.0 / 12.0
            e = at(aux, 0)
            slope_a = (8.0 * (at(aux, 0, 1) - at(aux, 0, -1)) - (at(aux, 0, 2) - at(aux, 0, -2))) * twelfth
            slope_b = (8.0 * (roll(e, -1, 2) - roll(e, 1, 2)) - (roll(e, -2, 2) - roll(e, 2, 2))) * twelfth
            v_e, v_w = at(state, 2, 1), at(state, 2, -1)
            turn_v = (8.0 * (v_e - v_w) - (at(state, 2, 2) - at(state, 2, -2))) * twelfth
            u_n, u_s = roll(u, -1, 2), roll(u, 1, 2)
            turn_u = (8.0 * (u_n - u_s) - (roll(u, -2, 2) - roll(u, 2, 2))) * twelfth
            spin = ((turn_v - turn_u) * inv_jac + at(stat.at[s, 1], 2)) * jac
            pair_u = at(state, 1, 1) + at(state, 1, -1)
            lap_u = (4.0 * (pair_u + (u_n + u_s)) + (roll(pair_u, -1, 2) + roll(pair_u, 1, 2)) - 20.0 * u) * (1.0 / 6.0)
            pair_v = v_e + v_w
            mid_v = 4.0 * v + pair_v
            lap_v = (4.0 * pair_v + (roll(mid_v, -1, 2) + roll(mid_v, 1, 2)) - 20.0 * v) * (1.0 / 6.0)
            u_t = spin * at(aux, 4) - slope_a + WAVE_SPEED * lap_u
            v_t = WAVE_SPEED * lap_v - spin * at(aux, 3) - slope_b
            for f, (x, x_t) in enumerate(((h, h_t), (u, u_t), (v, v_t))):
                new = x + TIME_STEP * x_t
                if now == 1:
                    new = 0.5 * (at(fresh, f) + new)
                fresh[f, :, rows, :] = new
            return carry
        lax.fori_loop(0, tile // ROWS2, step, 0)

    def tracer_pass(s, now):
        state, fresh = tra_of[now](s), tra_of[1 - now](s)

        def step(i, carry):
            r0 = pl.multiple_of(ROWSB * i, 8) + 8
            rows = pl.ds(r0, ROWSB)
            g = ghost_q[s, rows, :]
            mid, east, west, north, south = (coef[s, k, :, rows, :] for k in range(5))
            scale = area[s, 1, :, rows, :]
            lane = lanes(ROWSB)
            for t in range(fields):
                q = state[t, :, rows, :]
                q_e = state[t, :, pl.ds(r0 + 1, ROWSB), :]
                q_w = state[t, :, pl.ds(r0 - 1, ROWSB), :]
                x = jnp.stack(exchanged(q[0], q[1]))
                low = roll(g, -t, 1)
                high = roll(g, last_lane - TOP - t, 1)
                q_n, q_s = roll(x, -1, 2), roll(x, 1, 2)
                q_s = jnp.stack([jnp.where(lane == 0, low, q_s[0]), q_s[1]])
                q_n = jnp.stack([q_n[0], jnp.where(lane == last_lane, high, q_n[1])])
                total = mid * q + (east * q_e + west * q_w) + (north * q_n + south * q_s)
                new = q + scale * total
                if now == 1:
                    new = 0.5 * (fresh[t, :, rows, :] + new)
                fresh[t, :, rows, :] = new
            return carry
        lax.fori_loop(0, tile // ROWSB, step, 0)

    def stage(now, more):
        ends = unpack(dyn_of[now], BASE, DEPTH, of_dyn, now, ghost_d, True)
        unpack_corners(now, ends)

        def cells(s, carry):
            first_pass(s, now)
            second_pass(s, now)
            return carry
        lax.fori_loop(0, slots, cells, 0)

        def forward(send):
            if more is None:
                send(1 - now)
            else:
                pl.when(more)(lambda: send(1 - now))
        forward(pack_dyn)
        unpack(tra_of[now], fields, 1, of_tra, now, ghost_q, False)

        def tracers_of(s, carry):
            tracer_pass(s, now)
            return carry
        lax.fori_loop(0, slots, tracers_of, 0)
        forward(pack_tra)

    def one_step(step_index, carry):
        stage(0, None)
        stage(1, step_index < STEPS - 1)
        return carry

    lax.fori_loop(0, STEPS, one_step, 0)

    def give(src, dst):
        x0, x1 = src[0, inner, :], src[1, inner, :]
        dst[:, :LANES] = jnp.where(lanes(tile) < HALF, x0, x1)
        dst[:, LANES:] = x1[:, :tile - LANES]

    def give_tracer(t, carry):
        for s in range(slots):
            give(tra_a.at[s, t], out_q.at[t, s])
        return carry
    lax.fori_loop(0, fields, give_tracer, 0)

    def give_state(s, carry):
        for k, ref in enumerate((out_h, out_u, out_v)):
            give(dyn_a.at[s, k], ref.at[s])
        return carry
    lax.fori_loop(0, slots, give_state, 0)


def coefficients(rotation, pos_a, pos_b, count, tile):
    slots = rotation.shape[0]
    line = jnp.transpose(rotation, (0, 1, 3, 4, 2)).reshape(slots, 4, 4, rotation.shape[2])
    line = jnp.pad(line, ((0, 0), (0, 0), (0, 0), (2, LANES)))
    along = lambda part, pos: lax.dynamic_slice_in_dim(part, pos * tile, 2 * LANES, axis=3)
    line = jnp.concatenate([along(line[:, 0:2], pos_b), along(line[:, 2:4], pos_a)], axis=1)
    edge = jnp.stack([pos_a == 0, pos_a == count - 1, pos_b == 0, pos_b == count - 1])
    one = jnp.array([1.0, 0.0, 0.0, 1.0], F32)[:, None]
    line = jnp.where(edge[:, None, None], line, one)
    left = jnp.concatenate([line[..., 2:LANES], line[..., 0:2]], axis=-1)
    right = jnp.concatenate([line[..., LANES + 2:LANES + HALF], line[..., HALF:LANES + 2]], axis=-1)
    m = jnp.stack([left, right], axis=2)
    m = m.reshape(slots * 4, 2, 4, LANES)
    zero = jnp.zeros_like(m[:, :, 0])
    unit = jnp.ones_like(zero)
    m00, m01, m10, m11 = (m[:, :, k] for k in range(EDGES))
    stay = jnp.stack([unit, unit, m00, m00, m11, m11, zero, zero], axis=2)
    down = jnp.stack([zero, zero, zero, zero, m10, m10, zero, zero], axis=2)
    up = jnp.stack([zero, zero, m01, m01, zero, zero, zero, zero], axis=2)
    coef_e = jnp.stack([stay, down, up], axis=2)

    before, after = line[..., 1], line[..., tile + 2]
    found = []
    for k in range(EDGES):
        end_a, end_b = k // 2, k % 2
        by_a = (after if end_b else before)[:, end_a]
        by_b = (after if end_a else before)[:, 2 + end_b]
        found.append(jnp.where(edge[end_a], by_a, by_b))
    c = jnp.stack(found, axis=1).reshape(slots * 4, 4)
    zero = jnp.zeros_like(c[:, 0])
    rows = jnp.stack([jnp.stack([c[:, 0], c[:, 3]], -1), jnp.stack([zero, c[:, 2]], -1), jnp.stack([c[:, 1], zero], -1)], axis=1)
    rows = jnp.pad(rows, ((0, 0), (0, 0), (0, 6)))
    return coef_e, jnp.broadcast_to(rows[..., None], rows.shape + (LANES,))


def solution(mesh):
    cores, count = mesh.shape['panel'], mesh.shape['tx']
    slots = 6 // cores

    def body(height, wind_u, wind_v, sqrt_g, metric_aa, metric_ab, metric_bb, coriolis, topography, rotation, tracers):
        tile = height.shape[-1]
        fields = tracers.shape[0]
        coef_e, coef_c = coefficients(rotation, lax.axis_index('tx'), lax.axis_index('ty'), count, tile)
        rows = tile + DEPTH * TOP
        vmem = lambda *shape: pltpu.VMEM(shape, F32)
        blocks = (DEPTH, rows, LANES)
        state = [vmem(slots, count_f, *blocks) for count_f in (BASE, BASE, fields, fields)]
        messages = slots * EDGES
        buffers = [vmem(DEPTH + DEPTH, messages, DEPTH, TOP, LANES), vmem(DEPTH, messages, DEPTH, TOP, LANES),
                   vmem(DEPTH, messages, TOP, LANES)]
        counters = [pltpu.SemaphoreType.DMA((count_p,)) for count_p in (DEPTH + DEPTH, DEPTH, DEPTH)]
        whole = pl.BlockSpec(memory_space=pltpu.VMEM)
        args = (height, wind_u, wind_v, sqrt_g, metric_aa, metric_ab, metric_bb, coriolis, topography, coef_e, coef_c, tracers)
        outs = [jax.ShapeDtypeStruct(x.shape, F32) for x in (height, wind_u, wind_v, tracers)]
        call = pl.pallas_call(
            functools.partial(kernel, cores, count, tile),
            out_shape=outs,
            in_specs=[whole] * len(args),
            out_specs=[whole] * len(outs),
            scratch_shapes=state + [
                vmem(slots, DEPTH, BASE, *blocks), vmem(slots, DEPTH, *blocks),
                vmem(BASE + DEPTH, *blocks), vmem(slots, BASE + DEPTH, *blocks),
                vmem(DEPTH * LANES, LANES), vmem(DEPTH, LANES, LANES), vmem(slots, rows, LANES), vmem(slots, rows, LANES),
            ] + buffers * BASE + counters * DEPTH,
            compiler_params=pltpu.CompilerParams(
                collective_id=0, has_side_effects=True, vmem_limit_bytes=63 << 20),
            name='swe',
        )
        return tuple(call(*args))

    state_spec = P(('member', 'panel'), 'tx', 'ty')
    static_spec = P('panel', 'tx', 'ty')
    tracer_spec = P(None, ('member', 'panel'), 'tx', 'ty')
    in_specs = (state_spec, state_spec, state_spec, static_spec, static_spec, static_spec, static_spec, static_spec, static_spec, P('panel'), tracer_spec)
    out_specs = (state_spec, state_spec, state_spec, tracer_spec)
    return jax.shard_map(body, mesh=mesh, in_specs=in_specs, out_specs=out_specs, check_vma=False)
```

profile of v0, /device:TPU:97, one launch (start us, length us, event | category | flops | bytes accessed | tf_op | source)
XLA Modules:
  0.0 329.2 jit_solution(7395526808264107888)
XLA Ops:
  0.6 0.1 pad_add_fusion
  0.7 1.0 reshape.20
  1.8 0.2 pad_slice_fusion.1
  1.9 0.1 constant_dynamic-slice_fusion
  2.0 0.7 maximum_select_fusion
  2.8 0.2 slice_reduce_fusion.1
  3.0 0.1 slice.99
  3.1 0.1 slice.98
  3.2 0.1 pad_maximum_fusion.2
  3.3 0.1 slice.96
  3.4 0.1 pad_maximum_fusion.1
  3.5 0.1 fusion.3
  3.6 0.1 copy.39
  3.7 0.1 copy.41
  3.8 0.1 copy.40
  3.9 0.1 copy.42
  4.0 0.1 copy.43
  4.1 0.1 stack.85
  4.3 0.1 maximum_bitcast_fusion
  4.4 0.7 pad_maximum_fusion.coef_e
  5.1 0.8 broadcast_in_dim.26.coef_c
  5.9 312.6 %swe.1 = (f32[3,192,192]{2,1,0:T(8,128)}, f32[3,192,192]{2,1,0:T(8,128)}, f32[3,192,192]{2,1,0:T(8,128)}, f32[8,3,192,192]{3,2,1,0:T(8,128)}) custom-call(f32[3,192,192]{2,1,0:T(8,128)} %height.1, f32[3,192,192]{2,1,0:T(8,128)} %wind_u.1, f32[3,192,192]{2,1,0:T(8,128)} %wind_v.1, f32[3,192,192]{2,1,0:T(8,128)} %sqrt_g.1, f32[3,192,192]{2,1,0:T(8,128)} %metric_aa.1, ...), custom_call_target="tpu_custom_call" | custom-call | tf_op jit(solution)/shard_map/swe/pallas_call | solution.py:627
  318.5 1.9 copy.48
  320.4 1.9 copy.49
  322.3 1.9 copy.50
  324.3 5.0 %copy.51 = f32[8,3,192,192]{3,2,1,0:T(8,128)} copy(f32[8,3,192,192]{3,2,1,0:T(8,128)} %get-tuple-element.31) | data formatting | bytes 7077888
  (13 shorter events, 0.2 us)
where the time goes:
time: 330 us; the launch traced here: 329 us
  Pallas kernels  313 us (95%)
  local copies, waits for them, and re-layouts  13.9 us (4%)
    pallas_call x1, Pallas kernels, body(): return tuple(call(*args))  313 us
    unnamed x9, local copies, waits for them, and re-layouts  11.2 us

commit v1 on v0

--- a/solution.py
+++ b/solution.py
@@ -26,10 +26,11 @@
 EDGES = 4
 BASE = 3
 DEPTH = 2
-ROWS1 = 16
-ROWS2 = 16
-ROWSB = 32
-ROWSP = 32
+SPLIT = 32
+ROWS1, PARTS1 = 104, 1
+ROWS2, PARTS2 = 48, 1
+ROWSB, PARTSB = 16, 4
+ROWSP = 96
 F32 = jnp.float32
 
 
@@ -216,12 +217,12 @@
             packed = jnp.zeros((ROWSP, LANES), F32)
             for s in range(slots):
                 for f in range(count_f):
-                    low = DEPTH * TOP * s + depth * f
-                    high = low + TOP
-                    x = roll(src(s)[f, 0, rows, :], low, 1)
-                    packed = jnp.where((lane >= low) & (lane < low + depth), x, packed)
-                    x = roll(src(s)[f, 1, rows, :], high - last_lane + depth - 1, 1)
-                    packed = jnp.where((lane >= high) & (lane < high + depth), x, packed)
+                    low = TOP * s + depth * f
+                    high = low + tile - LANES - depth
+                    x = roll(jnp.where(lane < TOP, src(s)[f, 0, rows, :], src(s)[f, 1, rows, :]), low, 1)
+                    own = (lane >= low) & (lane < low + depth) | (lane >= high) & (lane < high + depth)
+                    packed = jnp.where(own, x, packed)
+            packed = jnp.where(lane < SPLIT, packed, roll(packed, depth, 1))
             pack[pl.ds(r0, ROWSP), :] = packed
             return carry
         lax.fori_loop(0, tile // ROWSP, step, 0)
@@ -229,7 +230,7 @@
         turned1 = jnp.transpose(pack[LANES:])
         for s in range(slots):
             for side in range(DEPTH):
-                g = TOP * (DEPTH * s + side)
+                g = TOP * s + (tile - LANES) * side
                 left = turned0[g:g + TOP]
                 right = jnp.where(lane8 < tile - LANES, turned1[g:g + TOP], left)
                 if side and depth == DEPTH:
@@ -262,7 +263,7 @@
                 mine = EDGES * s + k
                 start(of_end, par, mine, found[:-1] + (mix(lone[k], mine, found[-1]),), lone[k])
 
-    def unpack(dst, count_f, depth, kind, par, ghosts, turn):
+    def unpack(dst, count_f, depth, kind, par, ghosts, lean, turn):
         recv = kind[1]
         wait_for(kind, par)
         ends = {}
@@ -294,13 +295,15 @@
                 else:
                     if e == DEPTH and depth == DEPTH:
                         left, right = swap_pairs(left), swap_pairs(right)
-                    g = pl.ds(TOP * (DEPTH * s + e - DEPTH), TOP)
+                    g = pl.ds(TOP * s + (tile - LANES) * (e - DEPTH), TOP)
                     ghost_t[0, g, :] = jnp.where(lane8 < HALF, left, right)
                     ghost_t[1, g, :] = right
         low = jnp.transpose(ghost_t[0])
         high = jnp.transpose(ghost_t[1])[:tile - LANES]
-        for s in range(slots):
-            shift = -DEPTH * TOP * s
+        low = jnp.where(lanes(LANES) < SPLIT, low, roll(low, lean, 1))
+        high = jnp.where(lanes(tile - LANES) < SPLIT, high, roll(high, lean, 1))
+        for s in range(slots):
+            shift = -TOP * s
             ghosts[s, pl.ds(TOP, LANES), :] = roll(low, shift, 1)
             ghosts[s, pl.ds(TOP + LANES, tile - LANES), :] = roll(high, shift, 1)
         return ends
@@ -320,7 +323,7 @@
                 for f in range(1, BASE):
                     mirrored = jnp.broadcast_to(edge_row[DEPTH * f:DEPTH * f + 1, at:at + 1], (1, LANES))
                     value = jnp.where(alone, mirrored, x[f - 1:f])
-                    place = DEPTH * f + (TOP if end_b else 1)
+                    place = DEPTH * f + (tile - LANES + DEPTH if end_b else 1)
                     rows[end_a] = jnp.where(lane == place, value, rows[end_a])
             ghost_d[s, one(TOP - 1), :] = rows[0]
             ghost_d[s, one(tile + TOP), :] = rows[1]
@@ -333,8 +336,8 @@
     def with_columns(x, ghosts, low):
         left, right = exchanged(x[0], x[1])
         lane = lanes(left.shape[0])
-        left = jnp.where(lane >= LANES - 2, roll(ghosts, LANES - 2 - low, 1), left)
-        ghosts = roll(ghosts, tile - LANES - low - 8, 1)
+        ghosts = roll(ghosts, -DEPTH - low, 1)
+        left = jnp.where(lane >= LANES - DEPTH, ghosts, left)
         right = jnp.where((lane == tile - LANES) | (lane == tile - LANES + 1), ghosts, right)
         return jnp.stack([left, right])
 
@@ -390,7 +393,7 @@
     pack_tra(0)
 
     for par, group in groups:
-        unpack(group, BASE, DEPTH, of_dyn, par, ghost_d, False)
+        unpack(group, BASE, DEPTH, of_dyn, par, ghost_d, DEPTH, False)
         def fill_slot(s, carry):
             def fill(i, carry):
                 rows = pl.ds(pl.multiple_of(ROWSP * i, ROWSP) + 8, ROWSP)
@@ -405,11 +408,18 @@
             return lax.fori_loop(0, tile // ROWSP, fill, carry)
         lax.fori_loop(0, slots, fill_slot, 0)
 
+    def by_blocks(part, total, count_r, count_p):
+        def step(i, carry):
+            for k in range(count_p):
+                part(pl.multiple_of(count_r * count_p * i, TOP) + count_r * k)
+            return carry
+        lax.fori_loop(0, total // (count_r * count_p), step, 0)
+
     def first_pass(s, now):
         state = dyn_of[now](s)
 
-        def step(i, carry):
-            rows = pl.ds(pl.multiple_of(ROWS1 * i, ROWS1), ROWS1)
+        def part(r0):
+            rows = pl.ds(r0, ROWS1)
             g = ghost_d[s, rows, :]
             h, u, v = (with_columns(state[f, :, rows, :], g, 2 * f) for f in range(3))
             state[0, :, rows, :] = h
@@ -425,14 +435,13 @@
             aux[2, :, rows, :] = jh * contra_b
             aux[3, :, rows, :] = contra_a
             aux[4, :, rows, :] = contra_b
-            return carry
-        lax.fori_loop(0, (tile + 16) // ROWS1, step, 0)
+        by_blocks(part, tile + DEPTH * TOP, ROWS1, PARTS1)
 
     def second_pass(s, now):
         state, fresh = dyn_of[now](s), dyn_of[1 - now](s)
 
-        def step(i, carry):
-            r0 = pl.multiple_of(ROWS2 * i, 8) + 8
+        def part(r0):
+            r0 = r0 + TOP
 
             def at(ref, f, shift=0):
                 return ref[f, :, pl.ds(r0 + shift, ROWS2), :]
@@ -446,8 +455,9 @@
             flux_e = plus + (at(aux, 1, 1) - at(state, 0, 1))
             flux_w = (at(aux, 1, -1) + at(state, 0, -1)) + minus
             mass_b = at(aux, 2)
-            flux_n = (mass_b + h) + roll(mass_b - h, -1, 2)
-            flux_s = roll(flux_n, 1, 2)
+            plus_b, minus_b = mass_b + h, mass_b - h
+            flux_n = plus_b + roll(minus_b, -1, 2)
+            flux_s = roll(plus_b, 1, 2) + minus_b
             total = (flux_e - flux_w) + (flux_n - flux_s)
             h_t = (-0.5) * total * inv_jac
             coef[s, 0, :, rows, :] = 0.5 * total + 4.0
@@ -476,14 +486,13 @@
                 if now == 1:
                     new = 0.5 * (at(fresh, f) + new)
                 fresh[f, :, rows, :] = new
-            return carry
-        lax.fori_loop(0, tile // ROWS2, step, 0)
+        by_blocks(part, tile, ROWS2, PARTS2)
 
     def tracer_pass(s, now):
         state, fresh = tra_of[now](s), tra_of[1 - now](s)
 
-        def step(i, carry):
-            r0 = pl.multiple_of(ROWSB * i, 8) + 8
+        def part(r0):
+            r0 = r0 + TOP
             rows = pl.ds(r0, ROWSB)
             g = ghost_q[s, rows, :]
             mid, east, west, north, south = (coef[s, k, :, rows, :] for k in range(5))
@@ -494,21 +503,19 @@
                 q_e = state[t, :, pl.ds(r0 + 1, ROWSB), :]
                 q_w = state[t, :, pl.ds(r0 - 1, ROWSB), :]
                 x = jnp.stack(exchanged(q[0], q[1]))
-                low = roll(g, -t, 1)
-                high = roll(g, last_lane - TOP - t, 1)
+                ghost = roll(g, -t, 1)
                 q_n, q_s = roll(x, -1, 2), roll(x, 1, 2)
-                q_s = jnp.stack([jnp.where(lane == 0, low, q_s[0]), q_s[1]])
-                q_n = jnp.stack([q_n[0], jnp.where(lane == last_lane, high, q_n[1])])
+                q_s = jnp.stack([jnp.where(lane == 0, ghost, q_s[0]), q_s[1]])
+                q_n = jnp.stack([q_n[0], jnp.where(lane == last_lane, ghost, q_n[1])])
                 total = mid * q + (east * q_e + west * q_w) + (north * q_n + south * q_s)
                 new = q + scale * total
                 if now == 1:
                     new = 0.5 * (fresh[t, :, rows, :] + new)
                 fresh[t, :, rows, :] = new
-            return carry
-        lax.fori_loop(0, tile // ROWSB, step, 0)
+        by_blocks(part, tile, ROWSB, PARTSB)
 
     def stage(now, more):
-        ends = unpack(dyn_of[now], BASE, DEPTH, of_dyn, now, ghost_d, True)
+        ends = unpack(dyn_of[now], BASE, DEPTH, of_dyn, now, ghost_d, DEPTH, True)
         unpack_corners(now, ends)
 
         def cells(s, carry):
@@ -523,7 +530,7 @@
             else:
                 pl.when(more)(lambda: send(1 - now))
         forward(pack_dyn)
-        unpack(tra_of[now], fields, 1, of_tra, now, ghost_q, False)
+        unpack(tra_of[now], fields, 1, of_tra, now, ghost_q, -1, False)
 
         def tracers_of(s, carry):
             tracer_pass(s, now)

time: 330 us -> 217 us (0.66)
  Pallas kernels: 313 us -> 200 us
    pallas_call x1, Pallas kernels: 313 us -> 200 us  [body(): return tuple(call(*args))]
where the time goes in v1:
time: 217 us
  Pallas kernels  200 us (92%)
  local copies, waits for them, and re-layouts  13.9 us (6%)
    pallas_call x1, Pallas kernels, body(): return tuple(call(*args))  200 us
    unnamed x9, local copies, waits for them, and re-layouts  11.2 us

profile of v1, /device:TPU:97, one launch (start us, length us, event | category | flops | bytes accessed | tf_op | source)
XLA Modules:
  0.0 217.0 jit_solution(17986977063301521854)
XLA Ops:
  0.6 0.1 pad_add_fusion
  0.7 1.0 reshape.20
  1.8 0.2 pad_slice_fusion.1
  1.9 0.1 constant_dynamic-slice_fusion
  2.0 0.7 maximum_select_fusion
  2.8 0.2 slice_reduce_fusion.1
  3.0 0.1 slice.99
  3.1 0.1 slice.98
  3.2 0.1 pad_maximum_fusion.2
  3.3 0.1 slice.96
  3.4 0.1 pad_maximum_fusion.1
  3.5 0.1 fusion.3
  3.6 0.1 copy.39
  3.7 0.1 copy.41
  3.8 0.1 copy.40
  3.9 0.1 copy.42
  4.0 0.1 copy.43
  4.1 0.1 stack.85
  4.3 0.1 maximum_bitcast_fusion
  4.4 0.7 pad_maximum_fusion.coef_e
  5.1 0.8 broadcast_in_dim.26.coef_c
  5.9 200.4 %swe.1 = (f32[3,192,192]{2,1,0:T(8,128)}, f32[3,192,192]{2,1,0:T(8,128)}, f32[3,192,192]{2,1,0:T(8,128)}, f32[8,3,192,192]{3,2,1,0:T(8,128)}) custom-call(f32[3,192,192]{2,1,0:T(8,128)} %height.1, f32[3,192,192]{2,1,0:T(8,128)} %wind_u.1, f32[3,192,192]{2,1,0:T(8,128)} %wind_v.1, f32[3,192,192]{2,1,0:T(8,128)} %sqrt_g.1, f32[3,192,192]{2,1,0:T(8,128)} %metric_aa.1, ...), custom_call_target="tpu_custom_call" | custom-call | tf_op jit(solution)/shard_map/swe/pallas_call | solution.py:634
  206.3 1.9 copy.48
  208.2 1.9 copy.49
  210.1 1.9 copy.50
  212.0 5.0 %copy.51 = f32[8,3,192,192]{3,2,1,0:T(8,128)} copy(f32[8,3,192,192]{3,2,1,0:T(8,128)} %get-tuple-element.31) | data formatting | bytes 7077888
  (13 shorter events, 0.2 us)

commit v2 on v1

--- a/solution.py
+++ b/solution.py
@@ -328,22 +328,27 @@
             ghost_d[s, one(TOP - 1), :] = rows[0]
             ghost_d[s, one(tile + TOP), :] = rows[1]
 
-    def exchanged(left, right):
-        lane = lanes(left.shape[0])
-        return (jnp.where((lane == HALF) | (lane == HALF + 1), right, left),
-                jnp.where((lane == HALF - 1) | (lane == HALF - 2), left, right))
-
     def with_columns(x, ghosts, low):
-        left, right = exchanged(x[0], x[1])
-        lane = lanes(left.shape[0])
+        lane = lanes(x.shape[1])
         ghosts = roll(ghosts, -DEPTH - low, 1)
-        left = jnp.where(lane >= LANES - DEPTH, ghosts, left)
-        right = jnp.where((lane == tile - LANES) | (lane == tile - LANES + 1), ghosts, right)
+        left = jnp.where(lane >= LANES - DEPTH, ghosts, x[0])
+        right = jnp.where((lane == tile - LANES) | (lane == tile - LANES + 1), ghosts, x[1])
         return jnp.stack([left, right])
+
+    def refresh(state, count_f):
+        def step(f, carry):
+            for s in range(slots):
+                left, right = state(s)[f, 0, inner, :], state(s)[f, 1, inner, :]
+                lane = lanes(tile)
+                state(s)[f, 0, inner, :] = jnp.where(lane < HALF, left, right)
+                state(s)[f, 1, inner, :] = jnp.where((lane < HALF) & (lane >= tile - LANES), left, right)
+            return carry
+        lax.fori_loop(0, count_f, step, 0)
 
     def take(src, dst):
         dst[0, inner, :] = src[:, :LANES]
-        dst[1, inner, :] = roll(src[:, tile - LANES:], tile - LANES, 1)
+        dst[1, inner, :] = src[:, :LANES]
+        dst[1, inner, :tile - LANES] = src[:, LANES:]
 
     zero_rows = jnp.zeros((2 * LANES - tile, LANES), F32)
     pack[tile:2 * LANES, :] = zero_rows
@@ -502,9 +507,8 @@
                 q = state[t, :, rows, :]
                 q_e = state[t, :, pl.ds(r0 + 1, ROWSB), :]
                 q_w = state[t, :, pl.ds(r0 - 1, ROWSB), :]
-                x = jnp.stack(exchanged(q[0], q[1]))
                 ghost = roll(g, -t, 1)
-                q_n, q_s = roll(x, -1, 2), roll(x, 1, 2)
+                q_n, q_s = roll(q, -1, 2), roll(q, 1, 2)
                 q_s = jnp.stack([jnp.where(lane == 0, ghost, q_s[0]), q_s[1]])
                 q_n = jnp.stack([q_n[0], jnp.where(lane == last_lane, ghost, q_n[1])])
                 total = mid * q + (east * q_e + west * q_w) + (north * q_n + south * q_s)
@@ -539,6 +543,10 @@
         forward(pack_tra)
 
     def one_step(step_index, carry):
+        @pl.when(step_index == STEPS // DEPTH)
+        def _():
+            refresh(dyn_of[0], BASE)
+            refresh(tra_of[0], fields)
         stage(0, None)
         stage(1, step_index < STEPS - 1)
         return carry
@@ -573,7 +581,7 @@
     one = jnp.array([1.0, 0.0, 0.0, 1.0], F32)[:, None]
     line = jnp.where(edge[:, None, None], line, one)
     left = jnp.concatenate([line[..., 2:LANES], line[..., 0:2]], axis=-1)
-    right = jnp.concatenate([line[..., LANES + 2:LANES + HALF], line[..., HALF:LANES + 2]], axis=-1)
+    right = jnp.concatenate([line[..., LANES + 2:LANES + 2 + TOP * TOP + DEPTH], line[..., TOP * TOP + DEPTH + 2:LANES + 2]], axis=-1)
     m = jnp.stack([left, right], axis=2)
     m = m.reshape(slots * 4, 2, 4, LANES)
     zero = jnp.zeros_like(m[:, :, 0])

time: 217 us -> 213 us (0.982)
  Pallas kernels: 200 us -> 196 us
    pallas_call x1, Pallas kernels: 200 us -> 196 us  [body(): return tuple(call(*args))]
where the time goes in v2:
time: 213 us
  Pallas kernels  196 us (92%)
  local copies, waits for them, and re-layouts  13.9 us (7%)
    pallas_call x1, Pallas kernels, body(): return tuple(call(*args))  196 us
    unnamed x9, local copies, waits for them, and re-layouts  11.2 us

profile of v2, /device:TPU:97, one launch (start us, length us, event | category | flops | bytes accessed | tf_op | source)
XLA Modules:
  0.0 213.1 jit_solution(8053622165814139945)
XLA Ops:
  0.6 0.1 pad_add_fusion
  0.7 1.0 reshape.20
  1.8 0.2 pad_slice_fusion.1
  1.9 0.1 constant_dynamic-slice_fusion
  2.0 0.7 maximum_select_fusion
  2.8 0.2 slice_reduce_fusion.1
  3.0 0.1 slice.99
  3.1 0.1 slice.98
  3.2 0.1 pad_maximum_fusion.2
  3.3 0.1 slice.96
  3.4 0.1 pad_maximum_fusion.1
  3.5 0.1 fusion.3
  3.6 0.1 copy.39
  3.7 0.1 copy.41
  3.8 0.1 copy.40
  3.9 0.1 copy.42
  4.0 0.1 copy.43
  4.1 0.1 stack.85
  4.3 0.1 maximum_bitcast_fusion
  4.4 0.7 pad_maximum_fusion.coef_e
  5.1 0.8 broadcast_in_dim.26.coef_c
  5.9 196.5 %swe.1 = (f32[3,192,192]{2,1,0:T(8,128)}, f32[3,192,192]{2,1,0:T(8,128)}, f32[3,192,192]{2,1,0:T(8,128)}, f32[8,3,192,192]{3,2,1,0:T(8,128)}) custom-call(f32[3,192,192]{2,1,0:T(8,128)} %height.1, f32[3,192,192]{2,1,0:T(8,128)} %wind_u.1, f32[3,192,192]{2,1,0:T(8,128)} %wind_v.1, f32[3,192,192]{2,1,0:T(8,128)} %sqrt_g.1, f32[3,192,192]{2,1,0:T(8,128)} %metric_aa.1, ...), custom_call_target="tpu_custom_call" | custom-call | tf_op jit(solution)/shard_map/swe/pallas_call | solution.py:642
  202.4 1.9 copy.48
  204.3 1.9 copy.49
  206.2 1.9 copy.50
  208.1 5.0 %copy.51 = f32[8,3,192,192]{3,2,1,0:T(8,128)} copy(f32[8,3,192,192]{3,2,1,0:T(8,128)} %get-tuple-element.31) | data formatting | bytes 7077888
  (13 shorter events, 0.2 us)

commit v3 on v2

--- a/solution.py
+++ b/solution.py
@@ -136,8 +136,8 @@
 
 
 def kernel(cores, count, tile, height, wind_u, wind_v, sqrt_g, metric_aa, metric_ab, metric_bb, coriolis,
-           topography, coef_e, coef_c, tracers, out_h, out_u, out_v, out_q,
-           dyn_a, dyn_b, tra_a, tra_b, stat, area, aux, coef, pack, ghost_t, ghost_d, ghost_q,
+           topography, coef_e, coef_c, tracers, dyn_a, tra_a,
+           dyn_b, tra_b, stat, area, aux, coef, pack, ghost_t, ghost_d, ghost_q,
            *traffic):
     slots = 6 // cores
     fields = tracers.shape[0]
@@ -553,22 +553,18 @@
 
     lax.fori_loop(0, STEPS, one_step, 0)
 
+
+def finish(tile, dyn, tra, *outs):
     def give(src, dst):
-        x0, x1 = src[0, inner, :], src[1, inner, :]
-        dst[:, :LANES] = jnp.where(lanes(tile) < HALF, x0, x1)
-        dst[:, LANES:] = x1[:, :tile - LANES]
-
-    def give_tracer(t, carry):
-        for s in range(slots):
-            give(tra_a.at[s, t], out_q.at[t, s])
-        return carry
-    lax.fori_loop(0, fields, give_tracer, 0)
-
-    def give_state(s, carry):
-        for k, ref in enumerate((out_h, out_u, out_v)):
-            give(dyn_a.at[s, k], ref.at[s])
-        return carry
-    lax.fori_loop(0, slots, give_state, 0)
+        inner = pl.ds(TOP, tile)
+        left, right = src[0, inner, :], src[1, inner, :]
+        lane = lax.broadcasted_iota(jnp.int32, left.shape, 1)
+        dst[:, :LANES] = jnp.where(lane < HALF, left, right)
+        dst[:, LANES:] = right[:, :tile - LANES]
+    for k, out in enumerate(outs[:BASE]):
+        give(dyn.at[0, k], out.at[0])
+    for k in range(tra.shape[1]):
+        give(tra.at[0, k], outs[BASE].at[k, 0])
 
 
 def coefficients(rotation, pos_a, pos_b, count, tile):
@@ -617,19 +613,20 @@
         rows = tile + DEPTH * TOP
         vmem = lambda *shape: pltpu.VMEM(shape, F32)
         blocks = (DEPTH, rows, LANES)
-        state = [vmem(slots, count_f, *blocks) for count_f in (BASE, BASE, fields, fields)]
+        state = [vmem(slots, count_f, *blocks) for count_f in (BASE, fields)]
         messages = slots * EDGES
         buffers = [vmem(DEPTH + DEPTH, messages, DEPTH, TOP, LANES), vmem(DEPTH, messages, DEPTH, TOP, LANES),
                    vmem(DEPTH, messages, TOP, LANES)]
         counters = [pltpu.SemaphoreType.DMA((count_p,)) for count_p in (DEPTH + DEPTH, DEPTH, DEPTH)]
         whole = pl.BlockSpec(memory_space=pltpu.VMEM)
         args = (height, wind_u, wind_v, sqrt_g, metric_aa, metric_ab, metric_bb, coriolis, topography, coef_e, coef_c, tracers)
+        held = [jax.ShapeDtypeStruct((slots, count_f) + blocks, F32) for count_f in (BASE, fields)]
         outs = [jax.ShapeDtypeStruct(x.shape, F32) for x in (height, wind_u, wind_v, tracers)]
         call = pl.pallas_call(
             functools.partial(kernel, cores, count, tile),
-            out_shape=outs,
+            out_shape=held,
             in_specs=[whole] * len(args),
-            out_specs=[whole] * len(outs),
+            out_specs=[whole] * len(held),
             scratch_shapes=state + [
                 vmem(slots, DEPTH, BASE, *blocks), vmem(slots, DEPTH, *blocks),
                 vmem(BASE + DEPTH, *blocks), vmem(slots, BASE + DEPTH, *blocks),
@@ -639,7 +636,16 @@
                 collective_id=0, has_side_effects=True, vmem_limit_bytes=63 << 20),
             name='swe',
         )
-        return tuple(call(*args))
+        flat = pl.BlockSpec((1, tile, tile), lambda s: (s, 0, 0))
+        last = pl.pallas_call(
+            functools.partial(finish, tile),
+            out_shape=outs,
+            grid=(slots,),
+            in_specs=[pl.BlockSpec((1,) + x.shape[1:], lambda s: (s,) + (0,) * len(x.shape[1:])) for x in held],
+            out_specs=[flat] * BASE + [pl.BlockSpec((fields, 1, tile, tile), lambda s: (0, s, 0, 0))],
+            name='finish',
+        )
+        return tuple(last(*call(*args)))
 
     state_spec = P(('member', 'panel'), 'tx', 'ty')
     static_spec = P('panel', 'tx', 'ty')

time: 213 us -> 208 us (0.977)
  local copies, waits for them, and re-layouts: 13.9 us -> 3.21 us
  Pallas kernels: 196 us -> 202 us
    unnamed x9 -> x5, local copies, waits for them, and re-layouts: 11.2 us -> 0.47 us
    pallas_call x1 -> x2, Pallas kernels: 196 us -> 202 us  [body(): return tuple(last(*call(*args)))]
where the time goes in v3:
time: 208 us
  Pallas kernels  202 us (97%)
  local copies, waits for them, and re-layouts  3.21 us (2%)
    pallas_call x2, Pallas kernels, body(): return tuple(last(*call(*args)))  202 us

profile of v3, /device:TPU:97, one launch (start us, length us, event | category | flops | bytes accessed | tf_op | source)
XLA Modules:
  0.0 208.2 jit_solution(4831066609138139369)
XLA Ops:
  0.6 0.1 pad_add_fusion
  0.7 1.0 reshape.20
  1.8 0.2 pad_slice_fusion.1
  1.9 0.1 constant_dynamic-slice_fusion
  2.0 0.7 maximum_select_fusion
  2.8 0.2 slice_reduce_fusion.1
  3.0 0.1 slice.99
  3.1 0.1 slice.98
  3.2 0.1 pad_maximum_fusion.2
  3.3 0.1 slice.96
  3.4 0.1 pad_maximum_fusion.1
  3.5 0.1 fusion.3
  3.6 0.1 copy.39
  3.7 0.1 copy.41
  3.8 0.1 copy.40
  3.9 0.1 copy.42
  4.0 0.1 copy.43
  4.1 0.1 stack.85
  4.3 0.1 maximum_bitcast_fusion
  4.4 0.7 pad_maximum_fusion.coef_e
  5.1 0.8 broadcast_in_dim.26.coef_c
  5.9 195.8 %swe.1 = (f32[3,3,2,208,128]{4,3,2,1,0:T(8,128)}, f32[3,8,2,208,128]{4,3,2,1,0:T(8,128)}) custom-call(f32[3,192,192]{2,1,0:T(8,128)} %height.1, f32[3,192,192]{2,1,0:T(8,128)} %wind_u.1, f32[3,192,192]{2,1,0:T(8,128)} %wind_v.1, f32[3,192,192]{2,1,0:T(8,128)} %sqrt_g.1, f32[3,192,192]{2,1,0:T(8,128)} %metric_aa.1, f32[3,192,192]{2,1,0:T(8,128)} %metric_ab.1, ...), custom_call_target="tpu_custom_call" | custom-call | tf_op jit(solution)/shard_map/swe/pallas_call | solution.py:648
  201.7 6.5 %finish.1 = (f32[3,192,192]{2,1,0:T(8,128)}, f32[3,192,192]{2,1,0:T(8,128)}, f32[3,192,192]{2,1,0:T(8,128)}, f32[8,3,192,192]{3,2,1,0:T(8,128)}) custom-call(f32[3,3,2,208,128]{4,3,2,1,0:T(8,128)} %get-tuple-element.6.dyn, f32[3,8,2,208,128]{4,3,2,1,0:T(8,128)} %get-tuple-element.7.tra), custom_call_target="tpu_custom_call" | custom-call | tf_op jit(solution)/shard_map/finish/pallas_call | solution.py:648
  (13 shorter events, 0.2 us)

commit v4 on v3

--- a/solution.py
+++ b/solution.py
@@ -204,10 +204,13 @@
     def swap_pairs(x):
         return jnp.where(even8, roll(x, -1, 0), roll(x, 1, 0))
 
+    def send_edges(kind, par, which):
+        for s in range(slots):
+            for e in which:
+                start(kind, par, EDGES * s + e, edges[s][e], stays[s][e])
+
     def send_all(kind, par):
-        for s in range(slots):
-            for e in range(EDGES):
-                start(kind, par, EDGES * s + e, edges[s][e], stays[s][e])
+        send_edges(kind, par, range(EDGES))
 
     def pack_columns(src, count_f, depth, send, par):
         def step(i, carry):
@@ -379,15 +382,17 @@
         send_all(of_dyn, par)
 
     def pack_dyn(par):
+        send_corners(dyn_of[par], par)
+        pack_rows(dyn_of[par], BASE, DEPTH, of_dyn[0], par)
+        send_edges(of_dyn, par, range(DEPTH))
         pack_columns(dyn_of[par], BASE, DEPTH, of_dyn[0], par)
-        pack_rows(dyn_of[par], BASE, DEPTH, of_dyn[0], par)
-        send_all(of_dyn, par)
-        send_corners(dyn_of[par], par)
+        send_edges(of_dyn, par, range(DEPTH, EDGES))
 
     def pack_tra(par):
+        pack_rows(tra_of[par], fields, 1, of_tra[0], par)
+        send_edges(of_tra, par, range(DEPTH))
         pack_columns(tra_of[par], fields, 1, of_tra[0], par)
-        pack_rows(tra_of[par], fields, 1, of_tra[0], par)
-        send_all(of_tra, par)
+        send_edges(of_tra, par, range(DEPTH, EDGES))
 
     pack_dyn(0)
     def take_tracer(t, carry):

time: 208 us -> 209 us (level)
  no operation moved by 1% of the time
where the time goes in v4:
time: 209 us
  Pallas kernels  203 us (97%)
  local copies, waits for them, and re-layouts  3.21 us (2%)
    pallas_call x2, Pallas kernels, body(): return tuple(last(*call(*args)))  203 us

profile of v4, /device:TPU:97, one launch (start us, length us, event | category | flops | bytes accessed | tf_op | source)
XLA Modules:
  0.0 208.9 jit_solution(10588293425848333785)
XLA Ops:
  0.6 0.1 pad_add_fusion
  0.7 1.0 reshape.20
  1.8 0.2 pad_slice_fusion.1
  1.9 0.1 constant_dynamic-slice_fusion
  2.0 0.7 maximum_select_fusion
  2.8 0.2 slice_reduce_fusion.1
  3.0 0.1 slice.99
  3.1 0.1 slice.98
  3.2 0.1 pad_maximum_fusion.2
  3.3 0.1 slice.96
  3.4 0.1 pad_maximum_fusion.1
  3.5 0.1 fusion.3
  3.6 0.1 copy.39
  3.7 0.1 copy.41
  3.8 0.1 copy.40
  3.9 0.1 copy.42
  4.0 0.1 copy.43
  4.1 0.1 stack.85
  4.3 0.1 maximum_bitcast_fusion
  4.4 0.7 pad_maximum_fusion.coef_e
  5.1 0.8 broadcast_in_dim.26.coef_c
  5.9 196.5 %swe.1 = (f32[3,3,2,208,128]{4,3,2,1,0:T(8,128)}, f32[3,8,2,208,128]{4,3,2,1,0:T(8,128)}) custom-call(f32[3,192,192]{2,1,0:T(8,128)} %height.1, f32[3,192,192]{2,1,0:T(8,128)} %wind_u.1, f32[3,192,192]{2,1,0:T(8,128)} %wind_v.1, f32[3,192,192]{2,1,0:T(8,128)} %sqrt_g.1, f32[3,192,192]{2,1,0:T(8,128)} %metric_aa.1, f32[3,192,192]{2,1,0:T(8,128)} %metric_ab.1, ...), custom_call_target="tpu_custom_call" | custom-call | tf_op jit(solution)/shard_map/swe/pallas_call | solution.py:653
  202.4 6.5 %finish.1 = (f32[3,192,192]{2,1,0:T(8,128)}, f32[3,192,192]{2,1,0:T(8,128)}, f32[3,192,192]{2,1,0:T(8,128)}, f32[8,3,192,192]{3,2,1,0:T(8,128)}) custom-call(f32[3,3,2,208,128]{4,3,2,1,0:T(8,128)} %get-tuple-element.6.dyn, f32[3,8,2,208,128]{4,3,2,1,0:T(8,128)} %get-tuple-element.7.tra), custom_call_target="tpu_custom_call" | custom-call | tf_op jit(solution)/shard_map/finish/pallas_call | solution.py:653
  (13 shorter events, 0.2 us)

commit v5 on v3

--- a/solution.py
+++ b/solution.py
@@ -28,7 +28,7 @@
 DEPTH = 2
 SPLIT = 32
 ROWS1, PARTS1 = 104, 1
-ROWS2, PARTS2 = 48, 1
+ROWS2, PARTS2 = 32, 3
 ROWSB, PARTSB = 16, 4
 ROWSP = 96
 F32 = jnp.float32

time: 208 us -> 198 us (0.952)
  Pallas kernels: 202 us -> 192 us
    pallas_call x2, Pallas kernels: 202 us -> 192 us  [body(): return tuple(last(*call(*args)))]
where the time goes in v5:
time: 198 us
  Pallas kernels  192 us (97%)
  local copies, waits for them, and re-layouts  3.21 us (2%)
    pallas_call x2, Pallas kernels, body(): return tuple(last(*call(*args)))  192 us

profile of v5, /device:TPU:97, one launch (start us, length us, event | category | flops | bytes accessed | tf_op | source)
XLA Modules:
  0.0 197.7 jit_solution(362002433417825899)
XLA Ops:
  0.6 0.1 pad_add_fusion
  0.7 1.0 reshape.20
  1.8 0.2 pad_slice_fusion.1
  1.9 0.1 constant_dynamic-slice_fusion
  2.0 0.7 maximum_select_fusion
  2.8 0.2 slice_reduce_fusion.1
  3.0 0.1 slice.99
  3.1 0.1 slice.98
  3.2 0.1 pad_maximum_fusion.2
  3.3 0.1 slice.96
  3.4 0.1 pad_maximum_fusion.1
  3.5 0.1 fusion.3
  3.6 0.1 copy.39
  3.7 0.1 copy.41
  3.8 0.1 copy.40
  3.9 0.1 copy.42
  4.0 0.1 copy.43
  4.1 0.1 stack.85
  4.3 0.1 maximum_bitcast_fusion
  4.4 0.7 pad_maximum_fusion.coef_e
  5.1 0.8 broadcast_in_dim.26.coef_c
  5.9 185.3 %swe.1 = (f32[3,3,2,208,128]{4,3,2,1,0:T(8,128)}, f32[3,8,2,208,128]{4,3,2,1,0:T(8,128)}) custom-call(f32[3,192,192]{2,1,0:T(8,128)} %height.1, f32[3,192,192]{2,1,0:T(8,128)} %wind_u.1, f32[3,192,192]{2,1,0:T(8,128)} %wind_v.1, f32[3,192,192]{2,1,0:T(8,128)} %sqrt_g.1, f32[3,192,192]{2,1,0:T(8,128)} %metric_aa.1, f32[3,192,192]{2,1,0:T(8,128)} %metric_ab.1, ...), custom_call_target="tpu_custom_call" | custom-call | tf_op jit(solution)/shard_map/swe/pallas_call | solution.py:648
  191.2 6.5 %finish.1 = (f32[3,192,192]{2,1,0:T(8,128)}, f32[3,192,192]{2,1,0:T(8,128)}, f32[3,192,192]{2,1,0:T(8,128)}, f32[8,3,192,192]{3,2,1,0:T(8,128)}) custom-call(f32[3,3,2,208,128]{4,3,2,1,0:T(8,128)} %get-tuple-element.6.dyn, f32[3,8,2,208,128]{4,3,2,1,0:T(8,128)} %get-tuple-element.7.tra), custom_call_target="tpu_custom_call" | custom-call | tf_op jit(solution)/shard_map/finish/pallas_call | solution.py:648
  (13 shorter events, 0.2 us)
